TPU v7x, 32 devices: a whole 2x2x4 slice. The times are simulated.
32 devices in a mesh: mem: 4 (over x, core), ty: 2 (over y), tx: 4 (over z).
Axes of the slice: x: 2, y: 2, z: 4, core: 2. Of those that a mesh axis runs over, the one named last changes fastest.
Arguments:
- pressure: float32 [8, 50, 64, 512], P('mem', None, 'ty', 'tx'), may hold values from -6 to 6
- east_wind: float32 [8, 50, 64, 512], P('mem', None, 'ty', 'tx'), may hold values from -6 to 6
- north_wind: float32 [8, 50, 64, 512], P('mem', None, 'ty', 'tx'), may hold values from -6 to 6
- vertical_wind: float32 [8, 49, 64, 512], P('mem', None, 'ty', 'tx'), may hold values from -6 to 6
- sound_squared: float32 [50, 64, 512], P(None, 'ty', 'tx'), may hold values from 0.5 to 2
- thickness: float32 [50], replicated, may hold values from 0.05 to 0.5
- owner_map: int32 [8], replicated, may hold values from 0 to 7, each once
Outputs:
- analysis: float32 [2, 4, 6, 32, 128], P('ty', 'tx', None, 'mem')
Inputs may be any that keep to these rules, and one draw needn't show every extreme that they name: `owner_map`: every tile index appears exactly once.
All inputs are finite; a program needn't handle non-finite values.
Results may differ from a plain program's by a relative error of at most 0.0001.
Values sent between devices are 32-bit elements; how exact they have to be, the bound alone decides.
A program may use at most 128 MiB of HBM per device.

v0:
```python
import functools

import jax
import jax.numpy as jnp
from jax import lax
from jax.experimental import pallas as pl
from jax.experimental.pallas import tpu as pltpu
from jax.sharding import PartitionSpec as P

SUBSTEPS = 2
MESH = pl.DeviceIdType.MESH

horiz_ratio = 0.35
vert_ratio = 1.5


def unrolled(count, body, carry, most=7):
    width = max(d for d in range(1, most + 1) if count % d == 0)

    def block(i, c):
        for j in range(width):
            c = body(i * width + j, c)
        return c

    return lax.fori_loop(0, count // width, block, carry)


def kernel(
    sizes,
    p_hbm, u_hbm, v_hbm, w_hbm, s_hbm, thick_hbm, owner_hbm,
    out,
    p, u, v, w, s, inv, g, lam, sig, alpha, edge_cols, edge_rows,
    csend, crecv, rsend, rrecv, ueast, vnorth,
    integ, gath, everyone, thick, owner,
    load_sem, small_sem, cs_sem, cr_sem, rs_sem, rr_sem, ms_sem, mr_sem, as_sem, ar_sem,
):
    n_mem, n_ty, n_tx = sizes
    own, levels, rows, cols = p.shape
    quarter = rows // n_mem
    tiles = n_ty * n_tx
    mem, ty, tx = lax.axis_index("mem"), lax.axis_index("ty"), lax.axis_index("tx")
    me = ty * n_tx + tx
    east, west = {"tx": lax.rem(tx + 1, n_tx)}, {"tx": lax.rem(tx + n_tx - 1, n_tx)}
    north, south = {"ty": lax.rem(ty + 1, n_ty)}, {"ty": lax.rem(ty + n_ty - 1, n_ty)}
    lane = lax.broadcasted_iota(jnp.int32, (rows, cols), 1)
    row = lax.broadcasted_iota(jnp.int32, (rows, cols), 0)
    zero = jnp.zeros((rows, cols), jnp.float32)
    lane8 = lax.broadcasted_iota(jnp.int32, (8, cols), 1)
    zero8 = jnp.zeros((8, cols), jnp.float32)

    def load(src, dst, sem):
        copy = pltpu.make_async_copy(src, dst, load_sem.at[sem])
        copy.start()
        return copy

    small = [
        pltpu.make_async_copy(thick_hbm, thick, small_sem.at[0]),
        pltpu.make_async_copy(owner_hbm, owner, small_sem.at[1]),
    ]
    for copy in small:
        copy.start()
    loads = {}
    for m in range(own):
        for i, (name, src, dst) in enumerate((("p", p_hbm, p), ("u", u_hbm, u), ("v", v_hbm, v))):
            loads[name, m] = load(src.at[m], dst.at[m], 4 * m + i)
    loads["s"] = load(s_hbm, s, 4 * own)
    for m in range(own):
        loads["w", m] = load(w_hbm.at[m], w.at[m], 4 * m + 3)

    barrier = pltpu.get_barrier_semaphore()

    far = lambda d: -(min(d[0], n_ty - d[0]) + min(d[1], n_tx - d[1]))
    offsets = sorted([(a, b) for a in range(n_ty) for b in range(n_tx)], key=far)

    def tile_id(i):
        a, b = offsets[i - 1]
        other_ty, other_tx = lax.rem(ty + a, n_ty), lax.rem(tx + b, n_tx)
        return other_ty * n_tx + other_tx, {"ty": other_ty, "tx": other_tx}

    def mem_id(i):
        other = lax.rem(mem + i, n_mem)
        return other, {"mem": other}

    for i in range(1, tiles):
        pl.semaphore_signal(barrier, inc=1, device_id=tile_id(i)[1], device_id_type=MESH)
    for i in range(1, n_mem):
        pl.semaphore_signal(barrier, inc=1, device_id=mem_id(i)[1], device_id_type=MESH)

    def remote(src, dst, ssem, rsem, where):
        return pltpu.make_async_remote_copy(
            src_ref=src, dst_ref=dst, send_sem=ssem, recv_sem=rsem, device_id=where, device_id_type=MESH
        )

    def halo_copies(sub, m):
        kinds = ((0, east, north), (1, west, south))
        copies = []
        for kind, across, along in kinds:
            copies.append(remote(
                rsend.at[sub, m, kind], rrecv.at[sub, m, kind],
                rs_sem.at[sub, m, kind], rr_sem.at[sub, m, kind], along))
            copies.append(remote(
                csend.at[sub, m, kind], crecv.at[sub, m, kind],
                cs_sem.at[sub, m, kind], cr_sem.at[sub, m, kind], across))
        return copies

    def pack_first(k, x, packed):
        return jnp.where(lane == cols - 1 - k, pltpu.roll(x, cols - 1 - k, 1), packed)

    def pack_last(k, x, packed):
        shift = cols - k if not isinstance(k, int) or k > 0 else 0
        return jnp.where(lane == cols - 1 - k, pltpu.roll(x, shift, 1), packed)

    def pack_inputs(m):
        def one(k, c):
            last, first = c
            pk = p[m, k]
            first = pack_first(k, u[m, k] - horiz_ratio * pk, first)
            last = jnp.where(lane == cols - 1 - k, pltpu.roll(pk, lax.rem(cols - k, cols), 1), last)
            rsend[0, m, 0, pl.ds(k, 1), :] = p[m, k, rows - 1 : rows, :]
            rsend[0, m, 1, pl.ds(k, 1), :] = v[m, k, 0:1, :] - horiz_ratio * p[m, k, 0:1, :]
            return last, first

        packs = unrolled(levels, one, (zero, zero), 5)
        for kind in range(2):
            csend[0, m, kind] = packs[kind]

    def pivots():
        def one(i, c):
            k = i + 1
            below, gprev, mass_below, value = c
            sk = s[k]
            b = (vert_ratio * vert_ratio) * sk
            mass = thick[k] * sk
            r = 1.0 / (1.0 + b + below - below * gprev)
            gk = b * r
            value = (vert_ratio * (mass - mass_below) + below * value) * r
            inv[k] = r
            g[k] = gk
            lam[k] = value
            return b, gk, mass, value

        unrolled(levels - 1, one, ((vert_ratio * vert_ratio) * s[0], zero, thick[0] * s[0], zero))

        def weights(k, here, above, first, last, mass):
            mu = thick[k] - vert_ratio * (here - above)
            sk = (horiz_ratio * horiz_ratio) * mu * s[k]
            sig[k] = sk
            alpha[k] = mu - 4.0 * sk
            edge_rows[0, pl.ds(k, 1), :] = sk[0:1, :]
            edge_rows[1, pl.ds(k, 1), :] = sk[rows - 1 : rows, :]
            edge_rows[2, pl.ds(k, 1), :] = jnp.zeros((1, cols), jnp.float32) + thick[k]
            mass = jnp.where(lane8 == cols - 1 - k, thick[k], mass)
            return pack_first(k, sk, first), pack_last(k, sk, last), mass

        def two(i, c):
            k = levels - 1 - i
            here = lam[k] + g[k] * c[0]
            lam[k] = here
            return (here,) + weights(k, here, *c)

        c = unrolled(levels - 1, two, (zero, zero, zero, zero8))
        first, last, mass = weights(0, zero, *c)
        edge_cols[0] = first
        edge_cols[1] = last
        edge_cols[2] = jnp.concatenate([mass] * (rows // 8), axis=0)

    def forward(m):
        ueast[m] = crecv[0, m, 1] + horiz_ratio * csend[0, m, 0]
        vnorth[m] = rrecv[0, m, 1] + horiz_ratio * rsend[0, m, 0]

        def level(k, usum, vsum, dsum):
            pk = p[m, k]
            pw = jnp.where(lane == 0, pltpu.roll(crecv[0, m, 0], k + 1, 1), pltpu.roll(pk, 1, 1))
            ps = jnp.where(row == 0, rrecv[0, m, 0, pl.ds(k, 1), :], pltpu.roll(pk, 1, 0))
            uk = u[m, k] - horiz_ratio * (pk - pw)
            vk = v[m, k] - horiz_ratio * (pk - ps)
            ue = jnp.where(lane == cols - 1, pltpu.roll(ueast[m], k, 1), pltpu.roll(uk, cols - 1, 1))
            vn = jnp.where(row == rows - 1, vnorth[m, pl.ds(k, 1), :], pltpu.roll(vk, rows - 1, 0))
            div = (ue - uk) + (vn - vk)
            part = pk - horiz_ratio * s[k] * div
            p[m, k] = part
            return part, usum + thick[k] * uk, vsum + thick[k] * vk, dsum + sig[k] * div

        def one(i, c):
            k = i + 1
            part_below, value = c[:2]
            part, *sums = level(k, *c[2:])
            rhs = w[m, i] - vert_ratio * (part - part_below)
            value = (rhs + (vert_ratio * vert_ratio) * s[i] * value) * inv[k]
            w[m, i] = value
            return (part, value, *sums)

        part, *sums = level(0, zero, zero, zero)
        return unrolled(levels - 1, one, (part, zero, *sums))[2:]

    def backward(m):
        def finish(k, pk, last, first):
            p[m, k] = pk
            rsend[1, m, 0, pl.ds(k, 1), :] = pk[rows - 1 : rows, :]
            rsend[1, m, 1, pl.ds(k, 1), :] = pk[0:1, :]
            return pack_last(k, pk, last), pack_first(k, pk, first)

        def one(i, c):
            k = levels - 1 - i
            above = c[0]
            here = w[m, k - 1] + g[k] * above
            w[m, k - 1] = here
            pk = p[m, k] - vert_ratio * s[k] * (above - here)
            return (here,) + finish(k, pk, c[1], c[2])

        c = unrolled(levels - 1, one, (zero,) * 3)
        last, first = finish(0, p[m, 0] - vert_ratio * s[0] * c[0], c[1], c[2])
        csend[1, m, 0] = last
        csend[1, m, 1] = first

    def weigh(m):
        def level(k, mass, total):
            pk = p[m, k]
            around = (pltpu.roll(pk, 1, 1) + pltpu.roll(pk, cols - 1, 1)) + (
                pltpu.roll(pk, 1, 0) + pltpu.roll(pk, rows - 1, 0))
            return mass + thick[k] * pk, total + (alpha[k] * pk + sig[k] * around)

        def one(i, c):
            mass, total = level(i + 1, *c)
            return mass, total + lam[i + 1] * w[m, i]

        return unrolled(levels - 1, one, level(0, zero, zero))

    def integrals(m, usum, vsum, dsum, mass, total):
        across = lambda x: jnp.sum(x, axis=1, keepdims=True)
        along = lambda x: jnp.sum(x, axis=0, keepdims=True)
        pw, ps = crecv[1, m, 0], rrecv[1, m, 0]
        total = total - dsum / horiz_ratio
        total = total + jnp.where(lane == 0, across(edge_cols[0] * (pw - csend[1, m, 0])), 0.0)
        total = total + jnp.where(
            lane == cols - 1, across(edge_cols[1] * (crecv[1, m, 1] - csend[1, m, 1])), 0.0)
        total = total + jnp.where(row == 0, along(edge_rows[0] * (ps - rsend[1, m, 0])), 0.0)
        total = total + jnp.where(
            row == rows - 1, along(edge_rows[1] * (rrecv[1, m, 1] - rsend[1, m, 1])), 0.0)
        mass_west = jnp.where(lane == 0, across(edge_cols[2] * pw), pltpu.roll(mass, 1, 1))
        mass_south = jnp.where(row == 0, along(edge_rows[2] * ps), pltpu.roll(mass, 1, 0))
        return (
            total,
            usum - horiz_ratio * (mass - mass_west),
            vsum - horiz_ratio * (mass - mass_south),
        )

    sent = []

    def send_halos(sub, m):
        for copy in halo_copies(sub, m):
            copy.start()
            sent.append(copy)

    for m in range(own):
        for name in "puv":
            loads[name, m].wait()
        pack_inputs(m)
        if m == 0:
            pl.semaphore_wait(barrier, tiles - 1 + n_mem - 1)
        send_halos(0, m)
    loads["s"].wait()
    for copy in small:
        copy.wait()
    pivots()

    sums = []
    for m in range(own):
        loads["w", m].wait()
        for copy in halo_copies(0, m):
            copy.wait_recv()
        sums.append(forward(m))
        backward(m)
        send_halos(1, m)
    sums = [(*sums[m], *weigh(m)) for m in range(own)]
    for m in range(own):
        for copy in halo_copies(1, m):
            copy.wait_recv()
        for f, total in enumerate(integrals(m, *sums[m])):
            for q in range(n_mem):
                integ[m, q, f] = total[q * quarter : (q + 1) * quarter]
        for i in range(1, n_mem):
            other, where = mem_id(i)
            copy = remote(
                integ.at[m, other], gath.at[mem, m], ms_sem.at[m, other], mr_sem.at[m, mem], where)
            copy.start()
            sent.append(copy)

    fields = [[integ[m, mem, f] for f in range(3)] for m in range(own)]
    for m in range(own):
        for i in range(1, n_mem):
            other, where = mem_id(i)
            remote(integ.at[m, other], gath.at[other, m], ms_sem.at[m, other], mr_sem.at[m, other], where).wait_recv()
            fields.append([gath[other, m, f] for f in range(3)])
    members = len(fields)
    for f in range(3):
        total = fields[0][f]
        for one in fields[1:]:
            total = total + one[f]
        mean = total / members
        second = (fields[0][f] - mean) ** 2
        for one in fields[1:]:
            second = second + (one[f] - mean) ** 2
        everyone[me, f] = mean
        everyone[me, 3 + f] = second / (members - 1)

    for i in range(1, tiles):
        other, where = tile_id(i)
        copy = remote(everyone.at[me], everyone.at[me], as_sem.at[i], ar_sem.at[me], where)
        copy.start()
        sent.append(copy)
    mine = jnp.int32(0)
    for t in range(tiles):
        mine = jnp.where(owner[t] == me, t, mine)
    for i in range(1, tiles):
        other, where = tile_id(i)
        remote(everyone.at[me], everyone.at[other], as_sem.at[i], ar_sem.at[other], where).wait_recv()
    out[0, 0] = everyone[mine]
    for copy in sent:
        copy.wait_send()


def solution(mesh):
    n_mem, n_ty, n_tx = (mesh.shape[a] for a in ("mem", "ty", "tx"))
    tiles = n_ty * n_tx

    def local(pressure, east_wind, north_wind, vertical_wind, sound_squared, thickness, owner_map):
        own, levels, rows, cols = pressure.shape
        quarter = rows // n_mem
        f32 = jnp.float32
        dma = pltpu.SemaphoreType.DMA
        anywhere = pl.BlockSpec(memory_space=pl.ANY)
        return pl.pallas_call(
            functools.partial(kernel, (n_mem, n_ty, n_tx)),
            name="acoustic",
            out_shape=pltpu.VMEM((1, 1, 6, quarter, cols), f32),
            in_specs=[anywhere] * 7,
            out_specs=pl.BlockSpec(memory_space=pltpu.VMEM),
            scratch_shapes=[
                pltpu.VMEM((own, levels, rows, cols), f32),
                pltpu.VMEM((own, levels, rows, cols), f32),
                pltpu.VMEM((own, levels, rows, cols), f32),
                pltpu.VMEM((own, levels - 1, rows, cols), f32),
                *[pltpu.VMEM((levels, rows, cols), f32)] * 6,
                pltpu.VMEM((3, rows, cols), f32),
                pltpu.VMEM((3, levels, cols), f32),
                pltpu.VMEM((SUBSTEPS, own, 2, rows, cols), f32),
                pltpu.VMEM((SUBSTEPS, own, 2, rows, cols), f32),
                pltpu.VMEM((SUBSTEPS, own, 2, levels, cols), f32),
                pltpu.VMEM((SUBSTEPS, own, 2, levels, cols), f32),
                pltpu.VMEM((own, rows, cols), f32),
                pltpu.VMEM((own, levels, cols), f32),
                pltpu.VMEM((own, n_mem, 3, quarter, cols), f32),
                pltpu.VMEM((n_mem, own, 3, quarter, cols), f32),
                pltpu.VMEM((tiles, 6, quarter, cols), f32),
                pltpu.SMEM(thickness.shape, f32),
                pltpu.SMEM(owner_map.shape, jnp.int32),
                dma((4 * own + 1,)),
                dma((2,)),
                dma((SUBSTEPS, own, 2)),
                dma((SUBSTEPS, own, 2)),
                dma((SUBSTEPS, own, 2)),
                dma((SUBSTEPS, own, 2)),
                dma((own, n_mem)),
                dma((own, n_mem)),
                dma((tiles,)),
                dma((tiles,)),
            ],
            compiler_params=pltpu.CompilerParams(collective_id=0, has_side_effects=True),
        )(pressure, east_wind, north_wind, vertical_wind, sound_squared, thickness, owner_map)

    field = P("mem", None, "ty", "tx")
    return jax.shard_map(
        local,
        mesh=mesh,
        in_specs=(field, field, field, field, P(None, "ty", "tx"), P(), P()),
        out_specs=P("ty", "tx", None, "mem", None),
        check_vma=False,
    )
```

profile of v0, /device:TPU:0, one launch (start us, length us, event | category | flops | bytes accessed | tf_op | source)
XLA Modules:
  0.0 29.5 jit_solution(404657678348632176)
XLA Ops:
  0.0 28.8 %acoustic.1 = f32[1,1,6,8,128]{4,3,2,1,0:T(8,128)S(1)} custom-call(f32[2,50,32,128]{3,2,1,0:T(8,128)} %p_hbm.1, f32[2,50,32,128]{3,2,1,0:T(8,128)} %u_hbm.1, f32[2,50,32,128]{3,2,1,0:T(8,128)} %v_hbm.1, f32[2,49,32,128]{3,2,1,0:T(8,128)} %w_hbm.1, f32[50,32,128]{2,1,0:T(8,128)} %s_hbm.1, f32[50]{0:T(128)} %thick_hbm.1, s32[8]{0:T(128)} %owner_hbm.1), custom_call_target="tpu_custom_call" | custom-call | tf_op jit(solution)/shard_map/acoustic/pallas_call | solution.py:333
  28.8 0.6 %copy.9 = f32[1,1,6,8,128]{4,3,2,1,0:T(8,128)} copy(f32[1,1,6,8,128]{4,3,2,1,0:T(8,128)S(1)} %acoustic.1) | data formatting | bytes 49152
where the time goes:
time: 29.6 us; the launch traced here: 29.5 us
  Pallas kernels  28.8 us (97%)
  local copies, waits for them, and re-layouts  0.61 us (2%)
    pallas_call x1, Pallas kernels, local(): pl.pallas_call(functools.partial(kernel, (n_mem, n_ty, n_tx)), name='acou...  28.8 us
    unnamed x1, local copies, waits for them, and re-layouts  0.61 us

commit v1 on v0

v1 whole, which is shorter than its diff:
```python
import functools

import jax
import jax.numpy as jnp
from jax import lax
from jax.experimental import pallas as pl
from jax.experimental.pallas import tpu as pltpu
from jax.sharding import PartitionSpec as P

MESH = pl.DeviceIdType.MESH
PAD = 8

horiz_ratio = 0.35
vert_ratio = 1.5


def unrolled(count, body, carry, most=7):
    width = max(d for d in range(1, most + 1) if count % d == 0)

    def block(i, c):
        for j in range(width):
            c = body(i * width + j, c)
        return c

    return lax.fori_loop(0, count // width, block, carry)


def kernel(
    sizes,
    p_hbm, u_hbm, v_hbm, w_hbm, s_hbm, thick_hbm, owner_hbm,
    out,
    p, u, v, w, s, part, hs, vs, inv, binv, g, lam, mu, alpha, sig, sig_east, sig_west,
    edge, edge_recv, first_row, row_recv, sig_edge, sig_edge_recv, sig_rows, p_edge, p_rows,
    integ, gath, rim, rim_recv, lip, lip_recv, everyone, thick, owner,
    load_sem, small_sem, send_sem, member_sem, recv_sem,
):
    n_mem, n_ty, n_tx = sizes
    own, levels, rows, cols = u.shape
    quarter = rows // n_mem
    tiles = n_ty * n_tx
    body = pl.ds(PAD, rows)
    mem, ty, tx = lax.axis_index("mem"), lax.axis_index("ty"), lax.axis_index("tx")
    me = ty * n_tx + tx
    east, west = lax.rem(tx + 1, n_tx), lax.rem(tx + n_tx - 1, n_tx)
    north, south = lax.rem(ty + 1, n_ty), lax.rem(ty + n_ty - 1, n_ty)
    scope = jax.named_scope

    greet = {(i, 0, 0) for i in range(n_mem)} | {(0, a, b) for a in range(n_ty) for b in range(n_tx)}
    for i in range(n_mem):
        greet |= {(i, 0, 1 % n_tx), (i, 0, (n_tx - 1) % n_tx), (i, 1 % n_ty, 0), (i, (n_ty - 1) % n_ty, 0)}
    greet = sorted(greet - {(0, 0, 0)})
    barrier = pltpu.get_barrier_semaphore()
    for i, a, b in greet:
        where = {"mem": lax.rem(mem + i, n_mem), "ty": lax.rem(ty + a, n_ty), "tx": lax.rem(tx + b, n_tx)}
        pl.semaphore_signal(barrier, inc=1, device_id=where, device_id_type=MESH)

    def load(src, dst, sem):
        copy = pltpu.make_async_copy(src, dst, sem)
        copy.start()
        return copy

    loads = {}
    for m in range(own):
        loads["p", m] = load(p_hbm.at[m], p.at[m, :, body, :], load_sem.at[3 * m])
        loads["u", m] = load(u_hbm.at[m], u.at[m], load_sem.at[3 * m + 1])
        loads["v", m] = load(v_hbm.at[m], v.at[m, :, pl.ds(0, rows), :], load_sem.at[3 * m + 2])
        if m == 0:
            small = [load(thick_hbm, thick, small_sem.at[0]), load(owner_hbm, owner, small_sem.at[1])]
    loads["s"] = load(s_hbm, s, load_sem.at[3 * own])
    loads["w"] = load(w_hbm, w, load_sem.at[3 * own + 1])

    lane = lax.broadcasted_iota(jnp.int32, (rows, cols), 1)
    row = lax.broadcasted_iota(jnp.int32, (rows, cols), 0)
    lane8 = lax.broadcasted_iota(jnp.int32, (8, cols), 1)
    row8 = lax.broadcasted_iota(jnp.int32, (8, cols), 0)
    pair = lane >> 1
    even = (lane & 1) == 0
    is_first, is_last = lane == 0, lane == cols - 1
    is_edge = is_first | is_last
    zero = jnp.zeros((rows, cols), jnp.float32)
    blank = jnp.zeros((1, cols), jnp.float32)

    def to_west(x):
        return pltpu.roll(x, cols - 1, 1)

    def to_east(x):
        return pltpu.roll(x, 1, 1)

    def drain(ref, sem):
        pltpu.make_async_copy(ref, ref, sem).wait()

    def send(src, dst, kind, sem, where):
        pltpu.make_async_remote_copy(
            src_ref=src, dst_ref=dst, send_sem=send_sem.at[kind], recv_sem=sem, device_id=where, device_id_type=MESH
        ).start()

    def clear(k, c):
        for m in range(own):
            p[m, k, PAD - 1 : PAD, :] = blank
            p[m, k, PAD + rows : PAD + rows + 1, :] = blank
            v[m, k, rows : rows + 1, :] = blank
        sig[k, PAD - 1 : PAD, :] = blank
        sig[k, PAD + rows : PAD + rows + 1, :] = blank
        return c

    def pack(m):
        def one(k, packed):
            pk = p[m, k, body, :]
            ends = jnp.where(is_last, pk, u[m, k] - horiz_ratio * pk)
            first_row[m, pl.ds(k, 1), :] = v[m, k, 0:1, :] - horiz_ratio * p[m, k, PAD : PAD + 1, :]
            return jnp.where(pair == k, pltpu.roll(ends, 2 * k + 1, 1), packed)

        edge[m] = unrolled(levels, one, zero, 25)

    def pivots():
        def one(i, c):
            k = i + 1
            below, gprev, mass_below, value = c
            sk = s[k]
            hs[k] = horiz_ratio * sk
            vs[k] = vert_ratio * sk
            b = (vert_ratio * vert_ratio) * sk
            mass = thick[k] * sk
            r = 1.0 / (1.0 + b + below - below * gprev)
            gk = b * r
            bi = below * r
            value = (vert_ratio * (mass - mass_below)) * r + bi * value
            inv[k] = r
            binv[k] = bi
            g[k] = gk
            lam[k] = value
            return b, gk, mass, value

        s0 = s[0]
        hs[0] = horiz_ratio * s0
        vs[0] = vert_ratio * s0
        unrolled(levels - 1, one, ((vert_ratio * vert_ratio) * s0, zero, thick[0] * s0, zero))

        def weights(k, here, above, packed):
            mk = thick[k] - vert_ratio * (here - above)
            sk = (horiz_ratio * mk) * hs[k]
            mu[k] = mk
            sig[k, body, :] = sk
            sig_east[k] = to_west(sk)
            sig_west[k] = to_east(sk)
            alpha[k] = mk - 4.0 * sk
            return jnp.where(pair == k, pltpu.roll(sk, 2 * k + 1, 1), packed)

        def two(i, c):
            k = levels - 1 - i
            above, packed = c
            here = lam[k] + g[k] * above
            lam[k] = here
            return here, weights(k, here, above, packed)

        above, packed = unrolled(levels - 1, two, (zero, zero))
        sig_edge[...] = weights(0, zero, above, packed)

    def diverge(m):
        def one(k, c):
            usum, vsum, psum = c
            pk, uk, vk = p[m, k, body, :], u[m, k], v[m, k, pl.ds(0, rows), :]
            around = to_east(pk) + (p[m, k, pl.ds(PAD - 1, rows), :] + p[m, k, pl.ds(PAD + 1, rows), :])
            div = (to_west(uk - horiz_ratio * pk) - uk) + (v[m, k, pl.ds(1, rows), :] - vk)
            u[m, k] = div - horiz_ratio * (around - 4.0 * pk)
            tk = thick[k]
            return usum + tk * uk, vsum + tk * vk, psum + tk * pk

        return unrolled(levels, one, (zero, zero, zero), 10)

    def forward(m):
        mine = edge[m]
        halo = jnp.where(
            even, -horiz_ratio * (edge_recv[m, 0] - mine), pltpu.roll(edge_recv[m, 1] - mine, cols - 2, 1))

        def level(k, rest):
            hk = pltpu.roll(halo, lax.rem(cols - 2 * k, cols), 1)
            div = u[m, k] + jnp.where(is_edge, hk, 0.0)
            low = jnp.where(row8 == 0, -horiz_ratio * row_recv[m, 0, pl.ds(k, 1), :], 0.0)
            high = jnp.where(row8 == 7, row_recv[m, 1, pl.ds(k, 1), :], 0.0)
            div = jnp.concatenate([div[:8] + low, div[8 : rows - 8], div[rows - 8 :] + high], axis=0)
            e = hs[k] * div
            pa = p[m, k, body, :] - e
            part[m, k] = pa
            return pa, rest - mu[k] * e

        def one(i, c):
            k = i + 1
            pa_below, value, rest = c
            pa, rest = level(k, rest)
            rhs = w[m, i] - vert_ratio * (pa - pa_below)
            value = rhs * inv[k] + binv[k] * value
            w[m, i] = value
            return pa, value, rest

        pa, rest = level(0, zero)
        return unrolled(levels - 1, one, (pa, zero, rest))[2]

    def backward(m, rest):
        def weigh(k, pk, packed, mass, rest, te, tw, tn, ts):
            p_rows[m, 0, pl.ds(k, 1), :] = pk[0:1]
            p_rows[m, 1, pl.ds(k, 1), :] = pk[rows - 1 : rows]
            return (
                jnp.where(pair == k, pltpu.roll(pk, 2 * k + 1, 1), packed),
                mass + thick[k] * pk,
                rest + alpha[k] * pk,
                te + sig_east[k] * pk,
                tw + sig_west[k] * pk,
                tn + sig[k, pl.ds(PAD + 1, rows), :] * pk,
                ts + sig[k, pl.ds(PAD - 1, rows), :] * pk,
            )

        def one(i, c):
            k = levels - 1 - i
            above, packed, mass, rest, *sides = c
            here = w[m, k - 1] + g[k] * above
            pk = part[m, k] - vs[k] * (above - here)
            return (here, *weigh(k, pk, packed, mass, rest + lam[k] * here, *sides))

        above, *sums = unrolled(levels - 1, one, (zero, zero, zero, rest, zero, zero, zero, zero))
        packed, *sums = weigh(0, part[m, 0] - vs[0] * above, *sums)
        p_edge[m] = packed
        return sums

    def whole(m, usum, vsum, q, rest, te, tw, tn, ts):
        total = rest + jnp.where(is_first, 0.0, to_east(te)) + jnp.where(is_last, 0.0, to_west(tw))
        total = total + pltpu.roll(tn, 1, 0) + pltpu.roll(ts, rows - 1, 0)
        ue = usum - horiz_ratio * (q - jnp.where(is_first, 0.0, to_east(q)))
        vn = vsum - horiz_ratio * (q - jnp.where(row == 0, 0.0, pltpu.roll(q, 1, 0)))
        for r in range(n_mem):
            for f, x in enumerate((total, ue, vn)):
                integ[m, r, f] = x[r * quarter : (r + 1) * quarter]
        for i in range(1, n_mem):
            other = lax.rem(mem + i, n_mem)
            send(integ.at[m, other], gath.at[mem, m], 4, recv_sem.at[2], {"mem": other})

    def rims(qs):
        sig_e, sig_w = pltpu.roll(sig_edge_recv[1], cols - 1, 1), pltpu.roll(sig_edge_recv[0], 1, 1)
        rims = zero
        for m in range(own):
            te = jnp.sum(jnp.where(even, sig_e * p_edge[m], 0.0), axis=1, keepdims=True)
            tw = jnp.sum(jnp.where(even, 0.0, sig_w * p_edge[m]), axis=1, keepdims=True)
            rims = jnp.where(lane == 2 * m, te, rims)
            rims = jnp.where(lane == 2 * m + 1, pltpu.roll(qs[m], 2 * m + 2, 1), rims)
            rims = jnp.where(lane == cols - 1 - m, tw, rims)
        for r in range(n_mem):
            rim[r] = rims[r * quarter : (r + 1) * quarter]
        for i in range(n_mem):
            other = lax.rem(mem + i, n_mem)
            send(rim.at[other], rim_recv.at[0, mem], 5, recv_sem.at[3], {"mem": other, "tx": east})
            send(rim.at[other], rim_recv.at[1, mem], 5, recv_sem.at[3], {"mem": other, "tx": west})

    def lips(qs):
        for m in range(own):
            lip[m : m + 1, :] = jnp.sum(sig_rows[0] * p_rows[m, 1], axis=0, keepdims=True)
            lip[own + m : own + m + 1, :] = qs[m][rows - 1 : rows]
            lip[2 * own + m : 2 * own + m + 1, :] = jnp.sum(sig_rows[1] * p_rows[m, 0], axis=0, keepdims=True)
        send(lip, lip_recv.at[0, mem], 6, recv_sem.at[4], {"mem": 0, "ty": north})
        send(lip, lip_recv.at[1, mem], 6, recv_sem.at[4], {"mem": n_mem - 1, "ty": south})

    with scope("clear"):
        unrolled(levels, clear, 0, 10)
    for m in range(own):
        with scope(f"wait_load{m}"):
            for name in "puv":
                loads[name, m].wait()
        with scope(f"pack{m}"):
            pack(m)
    with scope("wait_barrier"):
        pl.semaphore_wait(barrier, len(greet))
    with scope("send"):
        for m in range(own):
            send(p.at[m, :, PAD + rows - 1, :], row_recv.at[m, 0], 0, member_sem.at[m, 0], {"ty": north})
            send(first_row.at[m], row_recv.at[m, 1], 0, member_sem.at[m, 0], {"ty": south})
            send(edge.at[m], edge_recv.at[m, 0], 1, member_sem.at[m, 1], {"tx": east})
            send(edge.at[m], edge_recv.at[m, 1], 1, member_sem.at[m, 1], {"tx": west})
    with scope("wait_s"):
        loads["s"].wait()
        for copy in small:
            copy.wait()
    with scope("pivots"):
        pivots()
    with scope("send_sig"):
        send(sig_edge, sig_edge_recv.at[0], 2, recv_sem.at[0], {"tx": east})
        send(sig_edge, sig_edge_recv.at[1], 2, recv_sem.at[0], {"tx": west})
        send(sig.at[:, PAD, :], sig_rows.at[0], 3, recv_sem.at[1], {"ty": south})
        send(sig.at[:, PAD + rows - 1, :], sig_rows.at[1], 3, recv_sem.at[1], {"ty": north})
    sums = []
    for m in range(own):
        with scope(f"diverge{m}"):
            sums.append(diverge(m))

    qs = []
    for m in range(own):
        with scope(f"wait_edge{m}"):
            if m == 0:
                loads["w"].wait()
            drain(edge_recv.at[m], member_sem.at[m, 1])
        with scope(f"wait_row{m}"):
            drain(row_recv.at[m], member_sem.at[m, 0])
        with scope(f"forward{m}"):
            rest = forward(m)
        with scope(f"backward{m}"):
            mass, *rest = backward(m, rest)
        qs.append(sums[m][2] + mass)
        if m == own - 1:
            with scope("wait_sig"):
                drain(sig_edge_recv, recv_sem.at[0])
            with scope("rims"):
                rims(qs)
        with scope(f"whole{m}"):
            whole(m, sums[m][0], sums[m][1], qs[m], *rest)
    with scope("wait_sig_rows"):
        drain(sig_rows, recv_sem.at[1])
    with scope("lips"):
        lips(qs)

    bottom = (row8[:quarter] == 0) & (mem == 0)
    top = (row8[:quarter] == quarter - 1) & (mem == n_mem - 1)
    with scope("wait_lip"):

        @pl.when((mem == 0) | (mem == n_mem - 1))
        def _():
            drain(lip_recv.at[0], recv_sem.at[4])

    with scope("wait_rim"):
        drain(rim_recv, recv_sem.at[3])
    with scope("wait_mem"):
        drain(gath.at[pl.ds(0, n_mem - 1)], recv_sem.at[2])

    with scope("stats"):
        fields = []
        lane_q = lane[:quarter]
        for i in range(n_mem):
            other = lax.rem(mem + i, n_mem)
            from_west, from_east = rim_recv[0, other], rim_recv[1, other]
            from_south, from_north = lip_recv[0, other], lip_recv[1, other]
            for m in range(own):
                source = integ.at[m, mem] if i == 0 else gath.at[other, m]
                total, ue, vn = (source[f] for f in range(3))
                te = from_west if m == 0 else pltpu.roll(from_west, cols - 2 * m, 1)
                tw = from_east if m == 0 else pltpu.roll(from_east, m, 1)
                total = total + jnp.where(lane_q == 0, te, 0.0) + jnp.where(lane_q == cols - 1, tw, 0.0)
                total = total + jnp.where(bottom, from_south[m : m + 1], 0.0)
                total = total + jnp.where(top, from_north[2 * own + m : 2 * own + m + 1], 0.0)
                ue = ue + horiz_ratio * jnp.where(lane_q == 0, pltpu.roll(from_west, cols - 2 * m - 1, 1), 0.0)
                vn = vn + horiz_ratio * jnp.where(bottom, from_south[own + m : own + m + 1], 0.0)
                fields.append([total, ue, vn])

        members = len(fields)
        for f in range(3):
            total = fields[0][f]
            for one in fields[1:]:
                total = total + one[f]
            mean = total / members
            second = (fields[0][f] - mean) ** 2
            for one in fields[1:]:
                second = second + (one[f] - mean) ** 2
            everyone[me, f] = mean
            everyone[me, 3 + f] = second / (members - 1)

        far = lambda d: -(min(d[0], n_ty - d[0]) + min(d[1], n_tx - d[1]))
        offsets = sorted([(a, b) for a in range(n_ty) for b in range(n_tx)], key=far)[:-1]
        for a, b in offsets:
            where = {"ty": lax.rem(ty + a, n_ty), "tx": lax.rem(tx + b, n_tx)}
            send(everyone.at[me], everyone.at[me], 7, recv_sem.at[5], where)
    mine = jnp.int32(0)
    for t in range(tiles):
        mine = jnp.where(owner[t] == me, t, mine)
    with scope("wait_all"):
        drain(everyone.at[pl.ds(0, tiles - 1)], recv_sem.at[5])
    with scope("finish"):
        out[0, 0] = everyone[mine]
        drain(row_recv, send_sem.at[0])
        drain(edge_recv, send_sem.at[1])
        drain(sig_edge_recv, send_sem.at[2])
        drain(sig_rows, send_sem.at[3])
        drain(gath.at[pl.ds(0, n_mem - 1)], send_sem.at[4])
        drain(rim_recv, send_sem.at[5])
        drain(lip_recv.at[0, pl.ds(0, 2)], send_sem.at[6])
        drain(everyone.at[pl.ds(0, tiles - 1)], send_sem.at[7])


def solution(mesh):
    n_mem, n_ty, n_tx = (mesh.shape[a] for a in ("mem", "ty", "tx"))
    tiles = n_ty * n_tx

    def local(pressure, east_wind, north_wind, vertical_wind, sound_squared, thickness, owner_map):
        own, levels, rows, cols = pressure.shape
        quarter = rows // n_mem
        f32 = jnp.float32
        dma = pltpu.SemaphoreType.DMA

        def vmem(*shape):
            return pltpu.VMEM(shape, f32)

        return pl.pallas_call(
            functools.partial(kernel, (n_mem, n_ty, n_tx)),
            name="acoustic",
            out_shape=pltpu.VMEM((1, 1, 6, quarter, cols), f32),
            in_specs=[pl.BlockSpec(memory_space=pl.ANY)] * 7,
            out_specs=pl.BlockSpec(memory_space=pltpu.VMEM),
            scratch_shapes=[
                vmem(own, levels, rows + 2 * PAD, cols),
                vmem(own, levels, rows, cols),
                vmem(own, levels, rows + PAD, cols),
                vmem(own, levels - 1, rows, cols),
                vmem(levels, rows, cols),
                vmem(own, levels, rows, cols),
                *[vmem(levels, rows, cols)] * 8,
                vmem(levels, rows + 2 * PAD, cols),
                *[vmem(levels, rows, cols)] * 2,
                vmem(own, rows, cols),
                vmem(own, 2, rows, cols),
                vmem(own, levels, cols),
                vmem(own, 2, levels, cols),
                vmem(rows, cols),
                vmem(2, rows, cols),
                vmem(2, levels, cols),
                vmem(own, rows, cols),
                vmem(own, 2, levels, cols),
                vmem(own, n_mem, 3, quarter, cols),
                vmem(n_mem, own, 3, quarter, cols),
                vmem(n_mem, quarter, cols),
                vmem(2, n_mem, quarter, cols),
                vmem(-(-3 * own // 8) * 8, cols),
                vmem(2, n_mem, -(-3 * own // 8) * 8, cols),
                vmem(tiles, 6, quarter, cols),
                pltpu.SMEM(thickness.shape, f32),
                pltpu.SMEM(owner_map.shape, jnp.int32),
                dma((3 * own + 2,)),
                dma((2,)),
                dma((8,)),
                dma((own, 2)),
                dma((6,)),
            ],
            compiler_params=pltpu.CompilerParams(collective_id=0, has_side_effects=True),
        )(pressure, east_wind, north_wind, vertical_wind, sound_squared, thickness, owner_map)

    field = P("mem", None, "ty", "tx")
    return jax.shard_map(
        local,
        mesh=mesh,
        in_specs=(field, field, field, field, P(None, "ty", "tx"), P(), P()),
        out_specs=P("ty", "tx", None, "mem", None),
        check_vma=False,
    )
```

time: 29.6 us -> 25.9 us (0.87)
  Pallas kernels: 28.8 us -> 25.1 us
    pallas_call x1, Pallas kernels: 28.8 us -> 25.1 us  [local(): pl.pallas_call(functools.partial(kernel, (n_mem, n_ty, n_tx)), name='acou...]
where the time goes in v1:
time: 25.9 us; the launch traced here: 25.7 us
  Pallas kernels  25.1 us (97%)
  local copies, waits for them, and re-layouts  0.61 us (2%)
    pallas_call x1, Pallas kernels, local(): pl.pallas_call(functools.partial(kernel, (n_mem, n_ty, n_tx)), name='acou...  25.1 us
    unnamed x1, local copies, waits for them, and re-layouts  0.61 us

profile of v1, /device:TPU:0, one launch (start us, length us, event | category | flops | bytes accessed | tf_op | source)
XLA Modules:
  0.0 25.7 jit_solution(3274306109013564141)
XLA Ops:
  0.0 25.1 %acoustic.1 = f32[1,1,6,8,128]{4,3,2,1,0:T(8,128)S(1)} custom-call(f32[2,50,32,128]{3,2,1,0:T(8,128)} %p_hbm.1, f32[2,50,32,128]{3,2,1,0:T(8,128)} %u_hbm.1, f32[2,50,32,128]{3,2,1,0:T(8,128)} %v_hbm.1, f32[2,49,32,128]{3,2,1,0:T(8,128)} %w_hbm.1, f32[50,32,128]{2,1,0:T(8,128)} %s_hbm.1, f32[50]{0:T(128)} %thick_hbm.1, s32[8]{0:T(128)} %owner_hbm.1), custom_call_target="tpu_custom_call" | custom-call | tf_op jit(solution)/shard_map/acoustic/pallas_call | solution.py:397
  25.1 0.6 %copy.9 = f32[1,1,6,8,128]{4,3,2,1,0:T(8,128)} copy(f32[1,1,6,8,128]{4,3,2,1,0:T(8,128)S(1)} %acoustic.1) | data formatting | bytes 49152

commit v2 on v1

--- a/solution.py
+++ b/solution.py
@@ -15,14 +15,18 @@
 
 
 def unrolled(count, body, carry, most=7):
-    width = max(d for d in range(1, most + 1) if count % d == 0)
+    trips = -(-count // most)
+    width = count // trips
+    first = count - trips * width
 
     def block(i, c):
         for j in range(width):
-            c = body(i * width + j, c)
+            c = body(first + i * width + j, c)
         return c
 
-    return lax.fori_loop(0, count // width, block, carry)
+    for i in range(first):
+        carry = body(i, carry)
+    return lax.fori_loop(0, trips, block, carry)
 
 
 def kernel(
@@ -59,14 +63,12 @@
         copy.start()
         return copy
 
-    loads = {}
+    loads = {"s": load(s_hbm, s, load_sem.at[3 * own])}
+    small = [load(thick_hbm, thick, small_sem.at[0]), load(owner_hbm, owner, small_sem.at[1])]
     for m in range(own):
         loads["p", m] = load(p_hbm.at[m], p.at[m, :, body, :], load_sem.at[3 * m])
         loads["u", m] = load(u_hbm.at[m], u.at[m], load_sem.at[3 * m + 1])
         loads["v", m] = load(v_hbm.at[m], v.at[m, :, pl.ds(0, rows), :], load_sem.at[3 * m + 2])
-        if m == 0:
-            small = [load(thick_hbm, thick, small_sem.at[0]), load(owner_hbm, owner, small_sem.at[1])]
-    loads["s"] = load(s_hbm, s, load_sem.at[3 * own])
     loads["w"] = load(w_hbm, w, load_sem.at[3 * own + 1])
 
     lane = lax.broadcasted_iota(jnp.int32, (rows, cols), 1)
@@ -136,6 +138,7 @@
         vs[0] = vert_ratio * s0
         unrolled(levels - 1, one, ((vert_ratio * vert_ratio) * s0, zero, thick[0] * s0, zero))
 
+    def adjoint():
         def weights(k, here, above, packed):
             mk = thick[k] - vert_ratio * (here - above)
             sk = (horiz_ratio * mk) * hs[k]
@@ -153,7 +156,7 @@
             lam[k] = here
             return here, weights(k, here, above, packed)
 
-        above, packed = unrolled(levels - 1, two, (zero, zero))
+        above, packed = unrolled(levels - 1, two, (zero, zero), 49)
         sig_edge[...] = weights(0, zero, above, packed)
 
     def diverge(m):
@@ -166,7 +169,7 @@
             tk = thick[k]
             return usum + tk * uk, vsum + tk * vk, psum + tk * pk
 
-        return unrolled(levels, one, (zero, zero, zero), 10)
+        return unrolled(levels, one, (zero, zero, zero), 50)
 
     def forward(m):
         mine = edge[m]
@@ -174,7 +177,7 @@
             even, -horiz_ratio * (edge_recv[m, 0] - mine), pltpu.roll(edge_recv[m, 1] - mine, cols - 2, 1))
 
         def level(k, rest):
-            hk = pltpu.roll(halo, lax.rem(cols - 2 * k, cols), 1)
+            hk = pltpu.roll(halo, cols - 2 * k if not isinstance(k, int) or k > 0 else 0, 1)
             div = u[m, k] + jnp.where(is_edge, hk, 0.0)
             low = jnp.where(row8 == 0, -horiz_ratio * row_recv[m, 0, pl.ds(k, 1), :], 0.0)
             high = jnp.where(row8 == 7, row_recv[m, 1, pl.ds(k, 1), :], 0.0)
@@ -194,7 +197,7 @@
             return pa, value, rest
 
         pa, rest = level(0, zero)
-        return unrolled(levels - 1, one, (pa, zero, rest))[2]
+        return unrolled(levels - 1, one, (pa, zero, rest), 49)[2]
 
     def backward(m, rest):
         def weigh(k, pk, packed, mass, rest, te, tw, tn, ts):
@@ -217,7 +220,7 @@
             pk = part[m, k] - vs[k] * (above - here)
             return (here, *weigh(k, pk, packed, mass, rest + lam[k] * here, *sides))
 
-        above, *sums = unrolled(levels - 1, one, (zero, zero, zero, rest, zero, zero, zero, zero))
+        above, *sums = unrolled(levels - 1, one, (zero, zero, zero, rest, zero, zero, zero, zero), 49)
         packed, *sums = weigh(0, part[m, 0] - vs[0] * above, *sums)
         p_edge[m] = packed
         return sums
@@ -260,26 +263,28 @@
 
     with scope("clear"):
         unrolled(levels, clear, 0, 10)
+    with scope("wait_s"):
+        loads["s"].wait()
+        for copy in small:
+            copy.wait()
+    with scope("pivots"):
+        pivots()
     for m in range(own):
         with scope(f"wait_load{m}"):
             for name in "puv":
                 loads[name, m].wait()
         with scope(f"pack{m}"):
             pack(m)
-    with scope("wait_barrier"):
-        pl.semaphore_wait(barrier, len(greet))
-    with scope("send"):
-        for m in range(own):
+        if m == 0:
+            with scope("wait_barrier"):
+                pl.semaphore_wait(barrier, len(greet))
+        with scope("send"):
             send(p.at[m, :, PAD + rows - 1, :], row_recv.at[m, 0], 0, member_sem.at[m, 0], {"ty": north})
             send(first_row.at[m], row_recv.at[m, 1], 0, member_sem.at[m, 0], {"ty": south})
             send(edge.at[m], edge_recv.at[m, 0], 1, member_sem.at[m, 1], {"tx": east})
             send(edge.at[m], edge_recv.at[m, 1], 1, member_sem.at[m, 1], {"tx": west})
-    with scope("wait_s"):
-        loads["s"].wait()
-        for copy in small:
-            copy.wait()
-    with scope("pivots"):
-        pivots()
+    with scope("adjoint"):
+        adjoint()
     with scope("send_sig"):
         send(sig_edge, sig_edge_recv.at[0], 2, recv_sem.at[0], {"tx": east})
         send(sig_edge, sig_edge_recv.at[1], 2, recv_sem.at[0], {"tx": west})

time: 25.9 us -> 23.6 us (0.911)
  Pallas kernels: 25.1 us -> 22.9 us
    pallas_call x1, Pallas kernels: 25.1 us -> 22.9 us  [local(): pl.pallas_call(functools.partial(kernel, (n_mem, n_ty, n_tx)), name='acou...]
where the time goes in v2:
time: 23.6 us; the launch traced here: 23.5 us
  Pallas kernels  22.9 us (97%)
  local copies, waits for them, and re-layouts  0.61 us (3%)
    pallas_call x1, Pallas kernels, local(): pl.pallas_call(functools.partial(kernel, (n_mem, n_ty, n_tx)), name='acou...  22.9 us
    unnamed x1, local copies, waits for them, and re-layouts  0.61 us

profile of v2, /device:TPU:0, one launch (start us, length us, event | category | flops | bytes accessed | tf_op | source)
XLA Modules:
  0.0 23.5 jit_solution(12630968189492206966)
XLA Ops:
  0.0 22.9 %acoustic.1 = f32[1,1,6,8,128]{4,3,2,1,0:T(8,128)S(1)} custom-call(f32[2,50,32,128]{3,2,1,0:T(8,128)} %p_hbm.1, f32[2,50,32,128]{3,2,1,0:T(8,128)} %u_hbm.1, f32[2,50,32,128]{3,2,1,0:T(8,128)} %v_hbm.1, f32[2,49,32,128]{3,2,1,0:T(8,128)} %w_hbm.1, f32[50,32,128]{2,1,0:T(8,128)} %s_hbm.1, f32[50]{0:T(128)} %thick_hbm.1, s32[8]{0:T(128)} %owner_hbm.1), custom_call_target="tpu_custom_call" | custom-call | tf_op jit(solution)/shard_map/acoustic/pallas_call | solution.py:402
  22.9 0.6 %copy.9 = f32[1,1,6,8,128]{4,3,2,1,0:T(8,128)} copy(f32[1,1,6,8,128]{4,3,2,1,0:T(8,128)S(1)} %acoustic.1) | data formatting | bytes 49152

commit v3 on v2

--- a/solution.py
+++ b/solution.py
@@ -29,19 +29,33 @@
     return lax.fori_loop(0, trips, block, carry)
 
 
+def layout(n_ty, n_tx):
+    homes = sorted({(0, 0), (n_ty // 2, n_tx // 2)})
+
+    def far(o, h):
+        a, b = (o[0] - h[0]) % n_ty, (o[1] - h[1]) % n_tx
+        return min(a, n_ty - a) + min(b, n_tx - b)
+
+    serve, hops = {}, set()
+    for o in ((a, b) for a in range(n_ty) for b in range(n_tx)):
+        n = min(range(len(homes)), key=lambda i: far(o, homes[i]))
+        serve[o] = n
+        hops.add(((o[0] - homes[n][0]) % n_ty, (o[1] - homes[n][1]) % n_tx))
+    return homes, serve, sorted(hops - {(0, 0)}, key=lambda d: (-far(d, (0, 0)), d))
+
+
 def kernel(
     sizes,
     p_hbm, u_hbm, v_hbm, w_hbm, s_hbm, thick_hbm, owner_hbm,
     out,
     p, u, v, w, s, part, hs, vs, inv, binv, g, lam, mu, alpha, sig, sig_east, sig_west,
     edge, edge_recv, first_row, row_recv, sig_edge, sig_edge_recv, sig_rows, p_edge, p_rows,
-    integ, gath, rim, rim_recv, lip, lip_recv, everyone, thick, owner,
-    load_sem, small_sem, send_sem, member_sem, recv_sem,
+    integ, gath, rim, rim_recv, lip, lip_recv, held, chosen, arrived, thick, owner,
+    load_sem, small_sem, send_sem, member_sem, recv_sem, round_sem,
 ):
     n_mem, n_ty, n_tx = sizes
     own, levels, rows, cols = u.shape
     quarter = rows // n_mem
-    tiles = n_ty * n_tx
     body = pl.ds(PAD, rows)
     mem, ty, tx = lax.axis_index("mem"), lax.axis_index("ty"), lax.axis_index("tx")
     me = ty * n_tx + tx
@@ -49,26 +63,56 @@
     north, south = lax.rem(ty + 1, n_ty), lax.rem(ty + n_ty - 1, n_ty)
     scope = jax.named_scope
 
-    greet = {(i, 0, 0) for i in range(n_mem)} | {(0, a, b) for a in range(n_ty) for b in range(n_tx)}
-    for i in range(n_mem):
-        greet |= {(i, 0, 1 % n_tx), (i, 0, (n_tx - 1) % n_tx), (i, 1 % n_ty, 0), (i, (n_ty - 1) % n_ty, 0)}
-    greet = sorted(greet - {(0, 0, 0)})
+    homes, serve, hops = layout(n_ty, n_tx)
+    sides = [(0, 1), (0, n_tx - 1), (1, 0), (n_ty - 1, 0)]
+
+    def shift(*offsets):
+        return sum(o[0] for o in offsets) % n_ty, sum(o[1] for o in offsets) % n_tx
+
+    def place(*offsets, **at):
+        a, b = shift(*offsets)
+        return {"ty": lax.rem(ty + a, n_ty), "tx": lax.rem(tx + b, n_tx), **at}
+
+    def member(i):
+        return {"mem": lax.rem(mem + i, n_mem)}
+
+    across, along = [place(o) for o in sides[:2]], [place(o) for o in sides[2:]]
+    others = [member(i) for i in range(1, n_mem)]
+    rounds = [across] * (n_tx // 2 - 1) + [along] * (n_ty // 2) + [others]
+
+    def greet(sem, peers):
+        for where in peers:
+            pl.semaphore_signal(sem, inc=1, device_id=where, device_id_type=MESH)
+
+    near = across + along + others
     barrier = pltpu.get_barrier_semaphore()
-    for i, a, b in greet:
-        where = {"mem": lax.rem(mem + i, n_mem), "ty": lax.rem(ty + a, n_ty), "tx": lax.rem(tx + b, n_tx)}
-        pl.semaphore_signal(barrier, inc=1, device_id=where, device_id_type=MESH)
+    greet(barrier, near)
+    met = []
+
+    def meet(more):
+        for _ in range(more):
+            n = len(met)
+            if n == 0:
+                pl.semaphore_wait(barrier, len(near))
+            elif n <= len(rounds):
+                pl.semaphore_wait(round_sem.at[n - 1], len(rounds[n - 1]))
+            if n < len(rounds):
+                greet(round_sem.at[n], rounds[n])
+            met.append(n)
 
     def load(src, dst, sem):
         copy = pltpu.make_async_copy(src, dst, sem)
         copy.start()
         return copy
 
-    loads = {"s": load(s_hbm, s, load_sem.at[3 * own])}
-    small = [load(thick_hbm, thick, small_sem.at[0]), load(owner_hbm, owner, small_sem.at[1])]
+    loads = {}
     for m in range(own):
         loads["p", m] = load(p_hbm.at[m], p.at[m, :, body, :], load_sem.at[3 * m])
-        loads["u", m] = load(u_hbm.at[m], u.at[m], load_sem.at[3 * m + 1])
-        loads["v", m] = load(v_hbm.at[m], v.at[m, :, pl.ds(0, rows), :], load_sem.at[3 * m + 2])
+        loads["v", m] = load(v_hbm.at[m], v.at[m, :, pl.ds(0, rows), :], load_sem.at[3 * m + 1])
+        loads["u", m] = load(u_hbm.at[m], u.at[m], load_sem.at[3 * m + 2])
+        if m == 0:
+            small = [load(thick_hbm, thick, small_sem.at[0]), load(owner_hbm, owner, small_sem.at[1])]
+            loads["s"] = load(s_hbm, s, load_sem.at[3 * own])
     loads["w"] = load(w_hbm, w, load_sem.at[3 * own + 1])
 
     lane = lax.broadcasted_iota(jnp.int32, (rows, cols), 1)
@@ -109,10 +153,16 @@
         def one(k, packed):
             pk = p[m, k, body, :]
             ends = jnp.where(is_last, pk, u[m, k] - horiz_ratio * pk)
+            return jnp.where(pair == k, pltpu.roll(ends, 2 * k + 1, 1), packed)
+
+        edge[m] = unrolled(levels, one, zero, 50)
+
+    def pack_rows(m):
+        def one(k, c):
             first_row[m, pl.ds(k, 1), :] = v[m, k, 0:1, :] - horiz_ratio * p[m, k, PAD : PAD + 1, :]
-            return jnp.where(pair == k, pltpu.roll(ends, 2 * k + 1, 1), packed)
-
-        edge[m] = unrolled(levels, one, zero, 25)
+            return c
+
+        unrolled(levels, one, 0, 50)
 
     def pivots():
         def one(i, c):
@@ -233,9 +283,12 @@
         for r in range(n_mem):
             for f, x in enumerate((total, ue, vn)):
                 integ[m, r, f] = x[r * quarter : (r + 1) * quarter]
-        for i in range(1, n_mem):
-            other = lax.rem(mem + i, n_mem)
-            send(integ.at[m, other], gath.at[mem, m], 4, recv_sem.at[2], {"mem": other})
+
+    def send_whole(m):
+        for n, h in reversed(list(enumerate(homes))):
+            for i in range(0 if n else 1, n_mem):
+                other = lax.rem(mem + i, n_mem)
+                send(integ.at[m, other], gath.at[n * n_mem + mem, m], 4, recv_sem.at[2], place(h, mem=other))
 
     def rims(qs):
         sig_e, sig_w = pltpu.roll(sig_edge_recv[1], cols - 1, 1), pltpu.roll(sig_edge_recv[0], 1, 1)
@@ -245,44 +298,60 @@
             tw = jnp.sum(jnp.where(even, 0.0, sig_w * p_edge[m]), axis=1, keepdims=True)
             rims = jnp.where(lane == 2 * m, te, rims)
             rims = jnp.where(lane == 2 * m + 1, pltpu.roll(qs[m], 2 * m + 2, 1), rims)
-            rims = jnp.where(lane == cols - 1 - m, tw, rims)
+            rims = jnp.where(lane == 2 * own + m, tw, rims)
+        rims = jnp.where(lane < 4 * own, rims, 0.0)
         for r in range(n_mem):
-            rim[r] = rims[r * quarter : (r + 1) * quarter]
-        for i in range(n_mem):
-            other = lax.rem(mem + i, n_mem)
-            send(rim.at[other], rim_recv.at[0, mem], 5, recv_sem.at[3], {"mem": other, "tx": east})
-            send(rim.at[other], rim_recv.at[1, mem], 5, recv_sem.at[3], {"mem": other, "tx": west})
+            piece = rims[r * quarter : (r + 1) * quarter]
+            piece = pltpu.roll(piece, 0, 1, stride=8, stride_axis=0)
+            rim[r] = jnp.sum(piece, axis=0, keepdims=True)
+
+    def send_rims():
+        for n, h in reversed(list(enumerate(homes))):
+            for i in range(n_mem):
+                other = lax.rem(mem + i, n_mem)
+                for kind in range(2):
+                    send(
+                        rim.at[other], rim_recv.at[n, kind, mem], 5, recv_sem.at[3],
+                        place(h, sides[kind], mem=other))
 
     def lips(qs):
         for m in range(own):
             lip[m : m + 1, :] = jnp.sum(sig_rows[0] * p_rows[m, 1], axis=0, keepdims=True)
             lip[own + m : own + m + 1, :] = qs[m][rows - 1 : rows]
             lip[2 * own + m : 2 * own + m + 1, :] = jnp.sum(sig_rows[1] * p_rows[m, 0], axis=0, keepdims=True)
-        send(lip, lip_recv.at[0, mem], 6, recv_sem.at[4], {"mem": 0, "ty": north})
-        send(lip, lip_recv.at[1, mem], 6, recv_sem.at[4], {"mem": n_mem - 1, "ty": south})
+
+    def send_lips():
+        for n, h in reversed(list(enumerate(homes))):
+            for kind, goal in enumerate((0, n_mem - 1)):
+                send(lip, lip_recv.at[kind, n, mem], 6, recv_sem.at[4], place(h, sides[2 + kind], mem=goal))
 
     with scope("clear"):
         unrolled(levels, clear, 0, 10)
-    with scope("wait_s"):
-        loads["s"].wait()
-        for copy in small:
-            copy.wait()
-    with scope("pivots"):
-        pivots()
     for m in range(own):
-        with scope(f"wait_load{m}"):
-            for name in "puv":
-                loads[name, m].wait()
+        with scope(f"wait_pv{m}"):
+            loads["p", m].wait()
+            loads["v", m].wait()
+        with scope(f"rows{m}"):
+            pack_rows(m)
+        if m == 0:
+            with scope("wait_barrier"):
+                meet(1)
+        with scope(f"send_rows{m}"):
+            send(p.at[m, :, PAD + rows - 1, :], row_recv.at[m, 0], 0, member_sem.at[m, 0], {"ty": north})
+            send(first_row.at[m], row_recv.at[m, 1], 0, member_sem.at[m, 0], {"ty": south})
+        with scope(f"wait_u{m}"):
+            loads["u", m].wait()
         with scope(f"pack{m}"):
             pack(m)
-        if m == 0:
-            with scope("wait_barrier"):
-                pl.semaphore_wait(barrier, len(greet))
-        with scope("send"):
-            send(p.at[m, :, PAD + rows - 1, :], row_recv.at[m, 0], 0, member_sem.at[m, 0], {"ty": north})
-            send(first_row.at[m], row_recv.at[m, 1], 0, member_sem.at[m, 0], {"ty": south})
             send(edge.at[m], edge_recv.at[m, 0], 1, member_sem.at[m, 1], {"tx": east})
             send(edge.at[m], edge_recv.at[m, 1], 1, member_sem.at[m, 1], {"tx": west})
+        if m == 0:
+            with scope("wait_s"):
+                loads["s"].wait()
+                for copy in small:
+                    copy.wait()
+            with scope("pivots"):
+                pivots()
     with scope("adjoint"):
         adjoint()
     with scope("send_sig"):
@@ -296,6 +365,8 @@
             sums.append(diverge(m))
 
     qs = []
+    with scope("meet0"):
+        meet(1)
     for m in range(own):
         with scope(f"wait_edge{m}"):
             if m == 0:
@@ -305,20 +376,31 @@
             drain(row_recv.at[m], member_sem.at[m, 0])
         with scope(f"forward{m}"):
             rest = forward(m)
+        with scope(f"meet{m + 1}"):
+            if m == 0:
+                meet(1)
+            else:
+                meet(len(rounds) + 1 - len(met))
+                send_whole(m - 1)
         with scope(f"backward{m}"):
             mass, *rest = backward(m, rest)
         qs.append(sums[m][2] + mass)
-        if m == own - 1:
+        last = m == own - 1
+        if last:
             with scope("wait_sig"):
+                meet(len(rounds) + 1 - len(met))
                 drain(sig_edge_recv, recv_sem.at[0])
-            with scope("rims"):
+                drain(sig_rows, recv_sem.at[1])
+        with scope(f"sums{m}"):
+            if last:
                 rims(qs)
-        with scope(f"whole{m}"):
+                lips(qs)
             whole(m, sums[m][0], sums[m][1], qs[m], *rest)
-    with scope("wait_sig_rows"):
-        drain(sig_rows, recv_sem.at[1])
-    with scope("lips"):
-        lips(qs)
+        with scope(f"send_sums{m}"):
+            if last:
+                send_rims()
+                send_lips()
+                send_whole(m)
 
     bottom = (row8[:quarter] == 0) & (mem == 0)
     top = (row8[:quarter] == quarter - 1) & (mem == n_mem - 1)
@@ -331,24 +413,30 @@
     with scope("wait_rim"):
         drain(rim_recv, recv_sem.at[3])
     with scope("wait_mem"):
-        drain(gath.at[pl.ds(0, n_mem - 1)], recv_sem.at[2])
-
-    with scope("stats"):
+        drain(gath.at[pl.ds(0, len(homes) * n_mem - 1)], recv_sem.at[2])
+
+    lane_q = lane[:quarter]
+
+    column_of = lane_q - 8 * row[:quarter]
+
+    def column(x, c):
+        return jnp.sum(jnp.where(column_of == c, x, 0.0), axis=1, keepdims=True)
+
+    def stats(n):
         fields = []
-        lane_q = lane[:quarter]
         for i in range(n_mem):
             other = lax.rem(mem + i, n_mem)
-            from_west, from_east = rim_recv[0, other], rim_recv[1, other]
-            from_south, from_north = lip_recv[0, other], lip_recv[1, other]
+            from_west, from_east = rim_recv[n, 0, other], rim_recv[n, 1, other]
+            from_south, from_north = lip_recv[0, n, other], lip_recv[1, n, other]
             for m in range(own):
-                source = integ.at[m, mem] if i == 0 else gath.at[other, m]
+                source = integ.at[m, mem] if n == 0 and i == 0 else gath.at[n * n_mem + other, m]
                 total, ue, vn = (source[f] for f in range(3))
-                te = from_west if m == 0 else pltpu.roll(from_west, cols - 2 * m, 1)
-                tw = from_east if m == 0 else pltpu.roll(from_east, m, 1)
+                te, qw = column(from_west, 2 * m), column(from_west, 2 * m + 1)
+                tw = column(from_east, 2 * own + m)
                 total = total + jnp.where(lane_q == 0, te, 0.0) + jnp.where(lane_q == cols - 1, tw, 0.0)
                 total = total + jnp.where(bottom, from_south[m : m + 1], 0.0)
                 total = total + jnp.where(top, from_north[2 * own + m : 2 * own + m + 1], 0.0)
-                ue = ue + horiz_ratio * jnp.where(lane_q == 0, pltpu.roll(from_west, cols - 2 * m - 1, 1), 0.0)
+                ue = ue + horiz_ratio * jnp.where(lane_q == 0, qw, 0.0)
                 vn = vn + horiz_ratio * jnp.where(bottom, from_south[own + m : own + m + 1], 0.0)
                 fields.append([total, ue, vn])
 
@@ -361,34 +449,53 @@
             second = (fields[0][f] - mean) ** 2
             for one in fields[1:]:
                 second = second + (one[f] - mean) ** 2
-            everyone[me, f] = mean
-            everyone[me, 3 + f] = second / (members - 1)
-
-        far = lambda d: -(min(d[0], n_ty - d[0]) + min(d[1], n_tx - d[1]))
-        offsets = sorted([(a, b) for a in range(n_ty) for b in range(n_tx)], key=far)[:-1]
-        for a, b in offsets:
-            where = {"ty": lax.rem(ty + a, n_ty), "tx": lax.rem(tx + b, n_tx)}
-            send(everyone.at[me], everyone.at[me], 7, recv_sem.at[5], where)
-    mine = jnp.int32(0)
-    for t in range(tiles):
-        mine = jnp.where(owner[t] == me, t, mine)
+            held[n, f] = mean
+            held[n, 3 + f] = second / (members - 1)
+
+    def number(o):
+        where = place(o)
+        return where["ty"] * n_tx + where["tx"]
+
+    def back(o):
+        return (-o[0] % n_ty, -o[1] % n_tx)
+
+    with scope("stats"):
+        for n in range(len(homes)):
+            stats(n)
+        for i, hop in enumerate(hops):
+            pick = jnp.int32(0)
+            for n, h in enumerate(homes):
+                if serve[shift(hop, h)] == n:
+                    pick = jnp.where(owner[number(back(h))] == number(hop), n, pick)
+            chosen[i] = held[pick]
+            send(chosen.at[i], arrived.at[i], 7, recv_sem.at[5], place(hop))
+        here, there, local = jnp.int32(0), jnp.int32(0), jnp.int32(0)
+        for o, n in serve.items():
+            found = owner[number(back(o))] == me
+            hop = shift(o, back(homes[n]))
+            if hop == (0, 0):
+                here = jnp.where(found, n, here)
+                local = jnp.where(found, 1, local)
+            else:
+                there = jnp.where(found, hops.index(hop), there)
     with scope("wait_all"):
-        drain(everyone.at[pl.ds(0, tiles - 1)], recv_sem.at[5])
+        drain(arrived, recv_sem.at[5])
     with scope("finish"):
-        out[0, 0] = everyone[mine]
+        out[0, 0] = jnp.where(local == 1, held[here], arrived[there])
         drain(row_recv, send_sem.at[0])
         drain(edge_recv, send_sem.at[1])
         drain(sig_edge_recv, send_sem.at[2])
         drain(sig_rows, send_sem.at[3])
-        drain(gath.at[pl.ds(0, n_mem - 1)], send_sem.at[4])
+        drain(gath.at[pl.ds(0, len(homes) * n_mem - 1)], send_sem.at[4])
         drain(rim_recv, send_sem.at[5])
-        drain(lip_recv.at[0, pl.ds(0, 2)], send_sem.at[6])
-        drain(everyone.at[pl.ds(0, tiles - 1)], send_sem.at[7])
+        drain(lip_recv.at[0, :, pl.ds(0, 2)], send_sem.at[6])
+        drain(arrived, send_sem.at[7])
 
 
 def solution(mesh):
     n_mem, n_ty, n_tx = (mesh.shape[a] for a in ("mem", "ty", "tx"))
-    tiles = n_ty * n_tx
+    homes, _, hops = layout(n_ty, n_tx)
+    rounds = n_tx // 2 + n_ty // 2
 
     def local(pressure, east_wind, north_wind, vertical_wind, sound_squared, thickness, owner_map):
         own, levels, rows, cols = pressure.shape
@@ -425,12 +532,14 @@
                 vmem(own, rows, cols),
                 vmem(own, 2, levels, cols),
                 vmem(own, n_mem, 3, quarter, cols),
-                vmem(n_mem, own, 3, quarter, cols),
-                vmem(n_mem, quarter, cols),
-                vmem(2, n_mem, quarter, cols),
+                vmem(len(homes) * n_mem, own, 3, quarter, cols),
+                vmem(n_mem, 1, cols),
+                vmem(len(homes), 2, n_mem, 1, cols),
                 vmem(-(-3 * own // 8) * 8, cols),
-                vmem(2, n_mem, -(-3 * own // 8) * 8, cols),
-                vmem(tiles, 6, quarter, cols),
+                vmem(2, len(homes), n_mem, -(-3 * own // 8) * 8, cols),
+                vmem(len(homes), 6, quarter, cols),
+                vmem(len(hops), 6, quarter, cols),
+                vmem(len(hops), 6, quarter, cols),
                 pltpu.SMEM(thickness.shape, f32),
                 pltpu.SMEM(owner_map.shape, jnp.int32),
                 dma((3 * own + 2,)),
@@ -438,6 +547,7 @@
                 dma((8,)),
                 dma((own, 2)),
                 dma((6,)),
+                pltpu.SemaphoreType.REGULAR((rounds,)),
             ],
             compiler_params=pltpu.CompilerParams(collective_id=0, has_side_effects=True),
         )(pressure, east_wind, north_wind, vertical_wind, sound_squared, thickness, owner_map)

time: 23.6 us -> 23.5 us (level)
  no operation moved by 1% of the time
where the time goes in v3:
time: 23.5 us; the launch traced here: 23.3 us
  Pallas kernels  22.7 us (97%)
  local copies, waits for them, and re-layouts  0.61 us (3%)
    pallas_call x1, Pallas kernels, local(): pl.pallas_call(functools.partial(kernel, (n_mem, n_ty, n_tx)), name='acou...  22.7 us
    unnamed x1, local copies, waits for them, and re-layouts  0.61 us

profile of v3, /device:TPU:0, one launch (start us, length us, event | category | flops | bytes accessed | tf_op | source)
XLA Modules:
  0.0 23.3 jit_solution(5692463240046286433)
XLA Ops:
  0.0 22.7 %acoustic.1 = f32[1,1,6,8,128]{4,3,2,1,0:T(8,128)S(1)} custom-call(f32[2,50,32,128]{3,2,1,0:T(8,128)} %p_hbm.1, f32[2,50,32,128]{3,2,1,0:T(8,128)} %u_hbm.1, f32[2,50,32,128]{3,2,1,0:T(8,128)} %v_hbm.1, f32[2,49,32,128]{3,2,1,0:T(8,128)} %w_hbm.1, f32[50,32,128]{2,1,0:T(8,128)} %s_hbm.1, f32[50]{0:T(128)} %thick_hbm.1, s32[8]{0:T(128)} %owner_hbm.1), custom_call_target="tpu_custom_call" | custom-call | tf_op jit(solution)/shard_map/acoustic/pallas_call | solution.py:509
  22.7 0.6 %copy.9 = f32[1,1,6,8,128]{4,3,2,1,0:T(8,128)} copy(f32[1,1,6,8,128]{4,3,2,1,0:T(8,128)S(1)} %acoustic.1) | data formatting | bytes 49152

commit v4 on v3

--- a/solution.py
+++ b/solution.py
@@ -30,7 +30,7 @@
 
 
 def layout(n_ty, n_tx):
-    homes = sorted({(0, 0), (n_ty // 2, n_tx // 2)})
+    homes = sorted({(0, 0), (n_ty // 2, 0)})
 
     def far(o, h):
         a, b = (o[0] - h[0]) % n_ty, (o[1] - h[1]) % n_tx
@@ -41,7 +41,10 @@
         n = min(range(len(homes)), key=lambda i: far(o, homes[i]))
         serve[o] = n
         hops.add(((o[0] - homes[n][0]) % n_ty, (o[1] - homes[n][1]) % n_tx))
-    return homes, serve, sorted(hops - {(0, 0)}, key=lambda d: (-far(d, (0, 0)), d))
+    sides = [(0, 1), (0, n_tx - 1), (1, 0), (n_ty - 1, 0)]
+    reach = max(far(((a + c) % n_ty, (b + d) % n_tx), (0, 0)) for a, b in homes for c, d in sides + [(0, 0)])
+    reach = max(reach, *(far(d, (0, 0)) for d in hops))
+    return homes, serve, sorted(hops - {(0, 0)}, key=lambda d: (-far(d, (0, 0)), d)), sides, reach
 
 
 def kernel(
@@ -63,8 +66,7 @@
     north, south = lax.rem(ty + 1, n_ty), lax.rem(ty + n_ty - 1, n_ty)
     scope = jax.named_scope
 
-    homes, serve, hops = layout(n_ty, n_tx)
-    sides = [(0, 1), (0, n_tx - 1), (1, 0), (n_ty - 1, 0)]
+    homes, serve, hops, sides, reach = layout(n_ty, n_tx)
 
     def shift(*offsets):
         return sum(o[0] for o in offsets) % n_ty, sum(o[1] for o in offsets) % n_tx
@@ -78,7 +80,7 @@
 
     across, along = [place(o) for o in sides[:2]], [place(o) for o in sides[2:]]
     others = [member(i) for i in range(1, n_mem)]
-    rounds = [across] * (n_tx // 2 - 1) + [along] * (n_ty // 2) + [others]
+    rounds = [across + along] * (reach - 1) + [others]
 
     def greet(sem, peers):
         for where in peers:
@@ -108,8 +110,8 @@
     loads = {}
     for m in range(own):
         loads["p", m] = load(p_hbm.at[m], p.at[m, :, body, :], load_sem.at[3 * m])
-        loads["v", m] = load(v_hbm.at[m], v.at[m, :, pl.ds(0, rows), :], load_sem.at[3 * m + 1])
-        loads["u", m] = load(u_hbm.at[m], u.at[m], load_sem.at[3 * m + 2])
+        loads["u", m] = load(u_hbm.at[m], u.at[m], load_sem.at[3 * m + 1])
+        loads["v", m] = load(v_hbm.at[m], v.at[m, :, pl.ds(0, rows), :], load_sem.at[3 * m + 2])
         if m == 0:
             small = [load(thick_hbm, thick, small_sem.at[0]), load(owner_hbm, owner, small_sem.at[1])]
             loads["s"] = load(s_hbm, s, load_sem.at[3 * own])
@@ -320,31 +322,45 @@
             lip[own + m : own + m + 1, :] = qs[m][rows - 1 : rows]
             lip[2 * own + m : 2 * own + m + 1, :] = jnp.sum(sig_rows[1] * p_rows[m, 0], axis=0, keepdims=True)
 
+    goals = (0, n_mem - 1)
+    kept = [sum(shift(h, sides[2 + kind]) == (0, 0) for h in homes) for kind in range(2)]
+
     def send_lips():
         for n, h in reversed(list(enumerate(homes))):
-            for kind, goal in enumerate((0, n_mem - 1)):
-                send(lip, lip_recv.at[kind, n, mem], 6, recv_sem.at[4], place(h, sides[2 + kind], mem=goal))
+            for kind, goal in enumerate(goals):
+                at = n * n_mem + mem
+                if shift(h, sides[2 + kind]) != (0, 0):
+                    send(lip, lip_recv.at[kind, at], 6, recv_sem.at[4], place(h, sides[2 + kind], mem=goal))
+                    continue
+
+                @pl.when(mem != goal)
+                def _():
+                    send(lip, lip_recv.at[kind, at], 8 + kind, recv_sem.at[4], {"mem": goal})
+
+                @pl.when(mem == goal)
+                def _():
+                    lip_recv[kind, at] = lip[...]
 
     with scope("clear"):
         unrolled(levels, clear, 0, 10)
     for m in range(own):
-        with scope(f"wait_pv{m}"):
+        with scope(f"wait_p{m}"):
             loads["p", m].wait()
-            loads["v", m].wait()
-        with scope(f"rows{m}"):
-            pack_rows(m)
         if m == 0:
             with scope("wait_barrier"):
                 meet(1)
-        with scope(f"send_rows{m}"):
+        with scope(f"wait_u{m}"):
             send(p.at[m, :, PAD + rows - 1, :], row_recv.at[m, 0], 0, member_sem.at[m, 0], {"ty": north})
-            send(first_row.at[m], row_recv.at[m, 1], 0, member_sem.at[m, 0], {"ty": south})
-        with scope(f"wait_u{m}"):
             loads["u", m].wait()
         with scope(f"pack{m}"):
             pack(m)
             send(edge.at[m], edge_recv.at[m, 0], 1, member_sem.at[m, 1], {"tx": east})
             send(edge.at[m], edge_recv.at[m, 1], 1, member_sem.at[m, 1], {"tx": west})
+        with scope(f"wait_v{m}"):
+            loads["v", m].wait()
+        with scope(f"rows{m}"):
+            pack_rows(m)
+            send(first_row.at[m], row_recv.at[m, 1], 0, member_sem.at[m, 0], {"ty": south})
         if m == 0:
             with scope("wait_s"):
                 loads["s"].wait()
@@ -363,10 +379,10 @@
     for m in range(own):
         with scope(f"diverge{m}"):
             sums.append(diverge(m))
+    with scope("meet0"):
+        meet(len(rounds) - 1)
 
     qs = []
-    with scope("meet0"):
-        meet(1)
     for m in range(own):
         with scope(f"wait_edge{m}"):
             if m == 0:
@@ -376,19 +392,15 @@
             drain(row_recv.at[m], member_sem.at[m, 0])
         with scope(f"forward{m}"):
             rest = forward(m)
-        with scope(f"meet{m + 1}"):
-            if m == 0:
-                meet(1)
-            else:
-                meet(len(rounds) + 1 - len(met))
-                send_whole(m - 1)
         with scope(f"backward{m}"):
             mass, *rest = backward(m, rest)
         qs.append(sums[m][2] + mass)
         last = m == own - 1
+        if m == 0:
+            with scope("meet"):
+                meet(len(rounds) + 1 - len(met))
         if last:
             with scope("wait_sig"):
-                meet(len(rounds) + 1 - len(met))
                 drain(sig_edge_recv, recv_sem.at[0])
                 drain(sig_rows, recv_sem.at[1])
         with scope(f"sums{m}"):
@@ -400,15 +412,17 @@
             if last:
                 send_rims()
                 send_lips()
-                send_whole(m)
+            send_whole(m)
 
     bottom = (row8[:quarter] == 0) & (mem == 0)
     top = (row8[:quarter] == quarter - 1) & (mem == n_mem - 1)
     with scope("wait_lip"):
 
-        @pl.when((mem == 0) | (mem == n_mem - 1))
-        def _():
-            drain(lip_recv.at[0], recv_sem.at[4])
+        for kind, goal in enumerate(goals):
+
+            @pl.when(mem == goal)
+            def _():
+                drain(lip_recv.at[kind, pl.ds(0, len(homes) * n_mem - kept[kind])], recv_sem.at[4])
 
     with scope("wait_rim"):
         drain(rim_recv, recv_sem.at[3])
@@ -427,7 +441,7 @@
         for i in range(n_mem):
             other = lax.rem(mem + i, n_mem)
             from_west, from_east = rim_recv[n, 0, other], rim_recv[n, 1, other]
-            from_south, from_north = lip_recv[0, n, other], lip_recv[1, n, other]
+            from_south, from_north = lip_recv[0, n * n_mem + other], lip_recv[1, n * n_mem + other]
             for m in range(own):
                 source = integ.at[m, mem] if n == 0 and i == 0 else gath.at[n * n_mem + other, m]
                 total, ue, vn = (source[f] for f in range(3))
@@ -488,14 +502,20 @@
         drain(sig_rows, send_sem.at[3])
         drain(gath.at[pl.ds(0, len(homes) * n_mem - 1)], send_sem.at[4])
         drain(rim_recv, send_sem.at[5])
-        drain(lip_recv.at[0, :, pl.ds(0, 2)], send_sem.at[6])
+        drain(lip_recv.at[0, pl.ds(0, 2 * len(homes) - kept[0] - kept[1])], send_sem.at[6])
+        for kind, goal in enumerate(goals):
+            if kept[kind]:
+
+                @pl.when(mem != goal)
+                def _():
+                    drain(lip_recv.at[0, pl.ds(0, kept[kind])], send_sem.at[8 + kind])
+
         drain(arrived, send_sem.at[7])
 
 
 def solution(mesh):
     n_mem, n_ty, n_tx = (mesh.shape[a] for a in ("mem", "ty", "tx"))
-    homes, _, hops = layout(n_ty, n_tx)
-    rounds = n_tx // 2 + n_ty // 2
+    homes, _, hops, _, reach = layout(n_ty, n_tx)
 
     def local(pressure, east_wind, north_wind, vertical_wind, sound_squared, thickness, owner_map):
         own, levels, rows, cols = pressure.shape
@@ -536,7 +556,7 @@
                 vmem(n_mem, 1, cols),
                 vmem(len(homes), 2, n_mem, 1, cols),
                 vmem(-(-3 * own // 8) * 8, cols),
-                vmem(2, len(homes), n_mem, -(-3 * own // 8) * 8, cols),
+                vmem(2, len(homes) * n_mem, -(-3 * own // 8) * 8, cols),
                 vmem(len(homes), 6, quarter, cols),
                 vmem(len(hops), 6, quarter, cols),
                 vmem(len(hops), 6, quarter, cols),
@@ -544,10 +564,10 @@
                 pltpu.SMEM(owner_map.shape, jnp.int32),
                 dma((3 * own + 2,)),
                 dma((2,)),
-                dma((8,)),
+                dma((10,)),
                 dma((own, 2)),
                 dma((6,)),
-                pltpu.SemaphoreType.REGULAR((rounds,)),
+                pltpu.SemaphoreType.REGULAR((reach,)),
             ],
             compiler_params=pltpu.CompilerParams(collective_id=0, has_side_effects=True),
         )(pressure, east_wind, north_wind, vertical_wind, sound_squared, thickness, owner_map)

time: 23.5 us -> 21.7 us (0.923)
  Pallas kernels: 22.7 us -> 20.9 us
    pallas_call x1, Pallas kernels: 22.7 us -> 20.9 us  [local(): pl.pallas_call(functools.partial(kernel, (n_mem, n_ty, n_tx)), name='acou...]
where the time goes in v4:
time: 21.7 us; the launch traced here: 21.6 us
  Pallas kernels  20.9 us (96%)
  local copies, waits for them, and re-layouts  0.61 us (3%)
    pallas_call x1, Pallas kernels, local(): pl.pallas_call(functools.partial(kernel, (n_mem, n_ty, n_tx)), name='acou...  20.9 us
    unnamed x1, local copies, waits for them, and re-layouts  0.61 us

profile of v4, /device:TPU:0, one launch (start us, length us, event | category | flops | bytes accessed | tf_op | source)
XLA Modules:
  0.0 21.6 jit_solution(17074176493095937483)
XLA Ops:
  0.0 20.9 %acoustic.1 = f32[1,1,6,8,128]{4,3,2,1,0:T(8,128)S(1)} custom-call(f32[2,50,32,128]{3,2,1,0:T(8,128)} %p_hbm.1, f32[2,50,32,128]{3,2,1,0:T(8,128)} %u_hbm.1, f32[2,50,32,128]{3,2,1,0:T(8,128)} %v_hbm.1, f32[2,49,32,128]{3,2,1,0:T(8,128)} %w_hbm.1, f32[50,32,128]{2,1,0:T(8,128)} %s_hbm.1, f32[50]{0:T(128)} %thick_hbm.1, s32[8]{0:T(128)} %owner_hbm.1), custom_call_target="tpu_custom_call" | custom-call | tf_op jit(solution)/shard_map/acoustic/pallas_call | solution.py:529
  20.9 0.6 %copy.9 = f32[1,1,6,8,128]{4,3,2,1,0:T(8,128)} copy(f32[1,1,6,8,128]{4,3,2,1,0:T(8,128)S(1)} %acoustic.1) | data formatting | bytes 49152

commit v5 on v4

--- a/solution.py
+++ b/solution.py
@@ -121,6 +121,7 @@
     row = lax.broadcasted_iota(jnp.int32, (rows, cols), 0)
     lane8 = lax.broadcasted_iota(jnp.int32, (8, cols), 1)
     row8 = lax.broadcasted_iota(jnp.int32, (8, cols), 0)
+    column_of = lane - 8 * lax.rem(row, quarter)
     pair = lane >> 1
     even = (lane & 1) == 0
     is_first, is_last = lane == 0, lane == cols - 1
@@ -191,39 +192,41 @@
         unrolled(levels - 1, one, ((vert_ratio * vert_ratio) * s0, zero, thick[0] * s0, zero))
 
     def adjoint():
-        def weights(k, here, above, packed):
+        def weights(k, here, above, packed, lean):
             mk = thick[k] - vert_ratio * (here - above)
             sk = (horiz_ratio * mk) * hs[k]
-            mu[k] = mk
+            ak = mk - 4.0 * sk
             sig[k, body, :] = sk
             sig_east[k] = to_west(sk)
             sig_west[k] = to_east(sk)
-            alpha[k] = mk - 4.0 * sk
-            return jnp.where(pair == k, pltpu.roll(sk, 2 * k + 1, 1), packed)
+            alpha[k] = ak
+            mu[k] = mk + ak
+            push = ak * vs[k]
+            lam[k + 1] = lean - push
+            return jnp.where(pair == k, pltpu.roll(sk, 2 * k + 1, 1), packed), here + push
 
         def two(i, c):
             k = levels - 1 - i
-            above, packed = c
+            above, packed, lean = c
             here = lam[k] + g[k] * above
-            lam[k] = here
-            return here, weights(k, here, above, packed)
-
-        above, packed = unrolled(levels - 1, two, (zero, zero), 49)
-        sig_edge[...] = weights(0, zero, above, packed)
+            return here, *weights(k, here, above, packed, lean)
+
+        above, packed, lean = unrolled(levels - 1, two, (zero, zero, zero), 49)
+        sig_edge[...] = weights(0, zero, above, packed, lean)[0]
 
     def diverge(m):
         def one(k, c):
-            usum, vsum, psum = c
+            usum, vsum, psum, rest = c
             pk, uk, vk = p[m, k, body, :], u[m, k], v[m, k, pl.ds(0, rows), :]
             around = to_east(pk) + (p[m, k, pl.ds(PAD - 1, rows), :] + p[m, k, pl.ds(PAD + 1, rows), :])
             div = (to_west(uk - horiz_ratio * pk) - uk) + (v[m, k, pl.ds(1, rows), :] - vk)
             u[m, k] = div - horiz_ratio * (around - 4.0 * pk)
             tk = thick[k]
-            return usum + tk * uk, vsum + tk * vk, psum + tk * pk
-
-        return unrolled(levels, one, (zero, zero, zero), 50)
-
-    def forward(m):
+            return usum + tk * uk, vsum + tk * vk, psum + tk * pk, rest + alpha[k] * pk
+
+        return unrolled(levels, one, (zero, zero, zero, zero), 50)
+
+    def forward(m, rest):
         mine = edge[m]
         halo = jnp.where(
             even, -horiz_ratio * (edge_recv[m, 0] - mine), pltpu.roll(edge_recv[m, 1] - mine, cols - 2, 1))
@@ -248,7 +251,7 @@
             w[m, i] = value
             return pa, value, rest
 
-        pa, rest = level(0, zero)
+        pa, rest = level(0, rest)
         return unrolled(levels - 1, one, (pa, zero, rest), 49)[2]
 
     def backward(m, rest):
@@ -258,7 +261,7 @@
             return (
                 jnp.where(pair == k, pltpu.roll(pk, 2 * k + 1, 1), packed),
                 mass + thick[k] * pk,
-                rest + alpha[k] * pk,
+                rest,
                 te + sig_east[k] * pk,
                 tw + sig_west[k] * pk,
                 tn + sig[k, pl.ds(PAD + 1, rows), :] * pk,
@@ -298,14 +301,11 @@
         for m in range(own):
             te = jnp.sum(jnp.where(even, sig_e * p_edge[m], 0.0), axis=1, keepdims=True)
             tw = jnp.sum(jnp.where(even, 0.0, sig_w * p_edge[m]), axis=1, keepdims=True)
-            rims = jnp.where(lane == 2 * m, te, rims)
-            rims = jnp.where(lane == 2 * m + 1, pltpu.roll(qs[m], 2 * m + 2, 1), rims)
-            rims = jnp.where(lane == 2 * own + m, tw, rims)
-        rims = jnp.where(lane < 4 * own, rims, 0.0)
+            q = jnp.sum(jnp.where(is_last, qs[m], 0.0), axis=1, keepdims=True)
+            for c, x in ((2 * m, te), (2 * m + 1, q), (2 * own + m, tw)):
+                rims = jnp.where(column_of == c, x, rims)
         for r in range(n_mem):
-            piece = rims[r * quarter : (r + 1) * quarter]
-            piece = pltpu.roll(piece, 0, 1, stride=8, stride_axis=0)
-            rim[r] = jnp.sum(piece, axis=0, keepdims=True)
+            rim[r] = jnp.sum(rims[r * quarter : (r + 1) * quarter], axis=0, keepdims=True)
 
     def send_rims():
         for n, h in reversed(list(enumerate(homes))):
@@ -346,16 +346,17 @@
     for m in range(own):
         with scope(f"wait_p{m}"):
             loads["p", m].wait()
+        with scope(f"wait_u{m}"):
+            loads["u", m].wait()
+        with scope(f"pack{m}"):
+            pack(m)
         if m == 0:
             with scope("wait_barrier"):
                 meet(1)
-        with scope(f"wait_u{m}"):
-            send(p.at[m, :, PAD + rows - 1, :], row_recv.at[m, 0], 0, member_sem.at[m, 0], {"ty": north})
-            loads["u", m].wait()
-        with scope(f"pack{m}"):
-            pack(m)
+        with scope(f"send{m}"):
             send(edge.at[m], edge_recv.at[m, 0], 1, member_sem.at[m, 1], {"tx": east})
             send(edge.at[m], edge_recv.at[m, 1], 1, member_sem.at[m, 1], {"tx": west})
+            send(p.at[m, :, PAD + rows - 1, :], row_recv.at[m, 0], 0, member_sem.at[m, 0], {"ty": north})
         with scope(f"wait_v{m}"):
             loads["v", m].wait()
         with scope(f"rows{m}"):
@@ -391,7 +392,7 @@
         with scope(f"wait_row{m}"):
             drain(row_recv.at[m], member_sem.at[m, 0])
         with scope(f"forward{m}"):
-            rest = forward(m)
+            rest = forward(m, sums[m][3])
         with scope(f"backward{m}"):
             mass, *rest = backward(m, rest)
         qs.append(sums[m][2] + mass)
@@ -431,10 +432,8 @@
 
     lane_q = lane[:quarter]
 
-    column_of = lane_q - 8 * row[:quarter]
-
     def column(x, c):
-        return jnp.sum(jnp.where(column_of == c, x, 0.0), axis=1, keepdims=True)
+        return jnp.sum(jnp.where(column_of[:quarter] == c, x, 0.0), axis=1, keepdims=True)
 
     def stats(n):
         fields = []
@@ -539,7 +538,7 @@
                 vmem(own, levels - 1, rows, cols),
                 vmem(levels, rows, cols),
                 vmem(own, levels, rows, cols),
-                *[vmem(levels, rows, cols)] * 8,
+                *[vmem(levels + 1, rows, cols)] * 8,
                 vmem(levels, rows + 2 * PAD, cols),
                 *[vmem(levels, rows, cols)] * 2,
                 vmem(own, rows, cols),

time: 21.7 us -> 21.6 us (level)
  no operation moved by 1% of the time
where the time goes in v5:
time: 21.6 us; the launch traced here: 21.4 us
  Pallas kernels  20.8 us (96%)
  local copies, waits for them, and re-layouts  0.61 us (3%)
    pallas_call x1, Pallas kernels, local(): pl.pallas_call(functools.partial(kernel, (n_mem, n_ty, n_tx)), name='acou...  20.8 us
    unnamed x1, local copies, waits for them, and re-layouts  0.61 us

profile of v5, /device:TPU:0, one launch (start us, length us, event | category | flops | bytes accessed | tf_op | source)
XLA Modules:
  0.0 21.4 jit_solution(5711864018078938083)
XLA Ops:
  0.0 20.8 %acoustic.1 = f32[1,1,6,8,128]{4,3,2,1,0:T(8,128)S(1)} custom-call(f32[2,50,32,128]{3,2,1,0:T(8,128)} %p_hbm.1, f32[2,50,32,128]{3,2,1,0:T(8,128)} %u_hbm.1, f32[2,50,32,128]{3,2,1,0:T(8,128)} %v_hbm.1, f32[2,49,32,128]{3,2,1,0:T(8,128)} %w_hbm.1, f32[50,32,128]{2,1,0:T(8,128)} %s_hbm.1, f32[50]{0:T(128)} %thick_hbm.1, s32[8]{0:T(128)} %owner_hbm.1), custom_call_target="tpu_custom_call" | custom-call | tf_op jit(solution)/shard_map/acoustic/pallas_call | solution.py:528
  20.8 0.6 %copy.9 = f32[1,1,6,8,128]{4,3,2,1,0:T(8,128)} copy(f32[1,1,6,8,128]{4,3,2,1,0:T(8,128)S(1)} %acoustic.1) | data formatting | bytes 49152

commit v6 on v5

--- a/solution.py
+++ b/solution.py
@@ -309,12 +309,11 @@
 
     def send_rims():
         for n, h in reversed(list(enumerate(homes))):
-            for i in range(n_mem):
-                other = lax.rem(mem + i, n_mem)
+            for goal in sorted(range(n_mem), key=lambda q: (q % 2, q)):
                 for kind in range(2):
                     send(
-                        rim.at[other], rim_recv.at[n, kind, mem], 5, recv_sem.at[3],
-                        place(h, sides[kind], mem=other))
+                        rim.at[goal], rim_recv.at[n, kind, mem], 5, recv_sem.at[3],
+                        place(h, sides[kind], mem=goal))
 
     def lips(qs):
         for m in range(own):
@@ -354,9 +353,9 @@
             with scope("wait_barrier"):
                 meet(1)
         with scope(f"send{m}"):
+            send(p.at[m, :, PAD + rows - 1, :], row_recv.at[m, 0], 0, member_sem.at[m, 0], {"ty": north})
             send(edge.at[m], edge_recv.at[m, 0], 1, member_sem.at[m, 1], {"tx": east})
             send(edge.at[m], edge_recv.at[m, 1], 1, member_sem.at[m, 1], {"tx": west})
-            send(p.at[m, :, PAD + rows - 1, :], row_recv.at[m, 0], 0, member_sem.at[m, 0], {"ty": north})
         with scope(f"wait_v{m}"):
             loads["v", m].wait()
         with scope(f"rows{m}"):
@@ -407,11 +406,11 @@
         with scope(f"sums{m}"):
             if last:
                 rims(qs)
+                send_rims()
                 lips(qs)
             whole(m, sums[m][0], sums[m][1], qs[m], *rest)
         with scope(f"send_sums{m}"):
             if last:
-                send_rims()
                 send_lips()
             send_whole(m)
 

time: 21.6 us -> 21.6 us (level)
  no operation moved by 1% of the time
where the time goes in v6:
time: 21.6 us; the launch traced here: 21.4 us
  Pallas kernels  20.8 us (96%)
  local copies, waits for them, and re-layouts  0.61 us (3%)
    pallas_call x1, Pallas kernels, local(): pl.pallas_call(functools.partial(kernel, (n_mem, n_ty, n_tx)), name='acou...  20.8 us
    unnamed x1, local copies, waits for them, and re-layouts  0.61 us

profile of v6, /device:TPU:0, one launch (start us, length us, event | category | flops | bytes accessed | tf_op | source)
XLA Modules:
  0.0 21.4 jit_solution(13033264806811141836)
XLA Ops:
  0.0 20.8 %acoustic.1 = f32[1,1,6,8,128]{4,3,2,1,0:T(8,128)S(1)} custom-call(f32[2,50,32,128]{3,2,1,0:T(8,128)} %p_hbm.1, f32[2,50,32,128]{3,2,1,0:T(8,128)} %u_hbm.1, f32[2,50,32,128]{3,2,1,0:T(8,128)} %v_hbm.1, f32[2,49,32,128]{3,2,1,0:T(8,128)} %w_hbm.1, f32[50,32,128]{2,1,0:T(8,128)} %s_hbm.1, f32[50]{0:T(128)} %thick_hbm.1, s32[8]{0:T(128)} %owner_hbm.1), custom_call_target="tpu_custom_call" | custom-call | tf_op jit(solution)/shard_map/acoustic/pallas_call | solution.py:527
  20.8 0.6 %copy.9 = f32[1,1,6,8,128]{4,3,2,1,0:T(8,128)} copy(f32[1,1,6,8,128]{4,3,2,1,0:T(8,128)S(1)} %acoustic.1) | data formatting | bytes 49152

commit v7 on v6

--- a/solution.py
+++ b/solution.py
@@ -379,8 +379,9 @@
     for m in range(own):
         with scope(f"diverge{m}"):
             sums.append(diverge(m))
-    with scope("meet0"):
-        meet(len(rounds) - 1)
+        if m == 0:
+            with scope("meet0"):
+                meet(len(rounds) - 1)
 
     qs = []
     for m in range(own):

time: 21.6 us -> 21.6 us (level)
  no operation moved by 1% of the time
where the time goes in v7:
time: 21.6 us; the launch traced here: 21.4 us
  Pallas kernels  20.8 us (96%)
  local copies, waits for them, and re-layouts  0.61 us (3%)
    pallas_call x1, Pallas kernels, local(): pl.pallas_call(functools.partial(kernel, (n_mem, n_ty, n_tx)), name='acou...  20.8 us
    unnamed x1, local copies, waits for them, and re-layouts  0.61 us

profile of v7, /device:TPU:0, one launch (start us, length us, event | category | flops | bytes accessed | tf_op | source)
XLA Modules:
  0.0 21.4 jit_solution(4155489791693279296)
XLA Ops:
  0.0 20.8 %acoustic.1 = f32[1,1,6,8,128]{4,3,2,1,0:T(8,128)S(1)} custom-call(f32[2,50,32,128]{3,2,1,0:T(8,128)} %p_hbm.1, f32[2,50,32,128]{3,2,1,0:T(8,128)} %u_hbm.1, f32[2,50,32,128]{3,2,1,0:T(8,128)} %v_hbm.1, f32[2,49,32,128]{3,2,1,0:T(8,128)} %w_hbm.1, f32[50,32,128]{2,1,0:T(8,128)} %s_hbm.1, f32[50]{0:T(128)} %thick_hbm.1, s32[8]{0:T(128)} %owner_hbm.1), custom_call_target="tpu_custom_call" | custom-call | tf_op jit(solution)/shard_map/acoustic/pallas_call | solution.py:528
  20.8 0.6 %copy.9 = f32[1,1,6,8,128]{4,3,2,1,0:T(8,128)} copy(f32[1,1,6,8,128]{4,3,2,1,0:T(8,128)S(1)} %acoustic.1) | data formatting | bytes 49152
